TPU v7x, 32 devices: a whole 2x2x4 slice. The times are simulated.
32 devices in a mesh: task: 4 (over y, core), col: 8 (over z, x).
Axes of the slice: x: 2, y: 2, z: 4, core: 2. Of those that a mesh axis runs over, the one named last changes fastest.
Arguments:
- layer_inputs: bfloat16 [4, 1024, 8192], P('task', None, 'col'), may hold values from -6 to 6
- queries: bfloat16 [4, 1024, 8192], P('task', None, 'col'), may hold values from -1000 to 1000, as said below
- key_values: bfloat16 [4, 1024, 2048], P('task', 'col'), may hold values from -8 to 8, as said below
- out_grads: bfloat16 [4, 1024, 8192], P('task', None, 'col'), may hold values from -0.29882812 to 0.29882812
- lengths: int32 [4, 4], P('task'), may hold values from 1 to 512, 1024 in all within a row
- task_weights: bfloat16 [4, 8192, 2048], P('task', 'col'), may hold values from -6 to 6
Outputs:
- fisher: float32 [4, 8192, 2048], P('task', 'col')
- merged: bfloat16 [8192, 2048], P('col')
Inputs may be any that keep to these rules, and one draw needn't show every extreme that they name: `queries`: queries of every head for the tokens of each task. `key_values`: keys and values of every head for the tokens of each task.
All inputs are finite; a program needn't handle non-finite values.
Results may differ from a plain program's by a relative error of at most 0.02.
Values may be sent and summed in bfloat16 or wider, within the bound.
No kernel may reach another device: no remote copies, remote signals or barrier semaphores. Data moves between devices by JAX's collectives and lax.ppermute only.
A program may use at most 128 MiB of HBM per device.

v0:
```python
import jax
import jax.numpy as jnp
from jax import lax
from jax.sharding import PartitionSpec as P

KVH = 8
HD = 128
EPS = 1e-06
NEGATIVE = -1e30


def layout(lengths, count):
    ending = jnp.cumsum(lengths)
    starts = ending - lengths
    places = jnp.arange(count, dtype=jnp.int32)
    owner = jnp.sum((places[:, None] >= ending[None, :]).astype(jnp.int32), axis=1)
    allowed = (owner[:, None] == owner[None, :]) & (places[:, None] >= places[None, :])
    return (owner, starts, allowed)


def head_grads(head_query, head_keys, head_values, head_cotangent, allowed):
    factor = HD ** (-0.5)
    scores = jnp.dot(head_query, head_keys.T, preferred_element_type=jnp.float32) * factor
    scores = jnp.where(allowed, scores, NEGATIVE)
    highest = jnp.max(scores, axis=1, keepdims=True)
    summed = jnp.sum(jnp.exp(scores - highest), axis=1, keepdims=True)
    chances = jnp.where(
        allowed, jnp.exp(scores - highest - jnp.log(summed)), jnp.zeros_like(scores)
    )
    slopes = jnp.dot(head_cotangent, head_values.T, preferred_element_type=jnp.float32)
    offsets = jnp.sum(chances * slopes, axis=1, keepdims=True)
    score_grads = (chances * (slopes - offsets)).astype(jnp.bfloat16)
    value_grads = jnp.dot(
        chances.astype(jnp.bfloat16).T, head_cotangent, preferred_element_type=jnp.float32
    )
    key_grads = jnp.dot(score_grads.T, head_query, preferred_element_type=jnp.float32) * factor
    return jnp.concatenate([key_grads, value_grads], axis=1)


def seq_fisher(inputs, grads_all, owner, starts, number_seqs):
    window = inputs.shape[0] // 2
    last_start = inputs.shape[0] - window

    def one_seq(running, number):
        opening = jnp.clip(starts[number], 0, last_start)
        rows_in = lax.dynamic_slice_in_dim(inputs, opening, window, 0)
        rows_grad = lax.dynamic_slice_in_dim(grads_all, opening, window, 0)
        inside = lax.dynamic_slice_in_dim(owner, opening, window, 0) == number
        rows_grad = jnp.where(inside[:, None], rows_grad, jnp.zeros_like(rows_grad))
        gradient = jnp.dot(rows_in.T, rows_grad, preferred_element_type=jnp.float32)
        return (running + gradient * gradient, None)

    start_value = jnp.zeros((inputs.shape[1], grads_all.shape[1]), jnp.float32)
    running, unused = lax.scan(one_seq, start_value, jnp.arange(number_seqs, dtype=jnp.int32))
    return running


def body(layer_inputs, queries, key_values, out_grads, lengths, task_weights):
    devices = lax.axis_size("col")
    groups = devices // KVH
    pair_width = 2 * HD
    kv_width = key_values.shape[2]
    inputs = layer_inputs[0]
    count = inputs.shape[0]
    local_rows = key_values[0]
    copies = jnp.repeat(local_rows.reshape(local_rows.shape[0], KVH, pair_width), groups, axis=1)
    head_block = lax.all_to_all(copies, "col", split_axis=1, concat_axis=0, tiled=True).reshape(
        count, pair_width
    )
    owner, starts, allowed = layout(lengths[0], count)
    head_keys = head_block[:, :HD]
    head_values = head_block[:, HD:]
    local_queries = queries[0]
    local_cotangents = out_grads[0]
    partial_sum = jnp.zeros((count, pair_width), jnp.float32)
    for member in range(local_queries.shape[1] // HD):
        head_query = local_queries[:, member * HD : (member + 1) * HD]
        head_cotangent = local_cotangents[:, member * HD : (member + 1) * HD]
        partial_sum = partial_sum + head_grads(
            head_query, head_keys, head_values, head_cotangent, allowed
        )
    partial_value = partial_sum.astype(jnp.bfloat16)
    piece = lax.all_gather(partial_value, "col", axis=1, tiled=True)
    shards = piece.shape[1] // pair_width
    owners = jnp.arange(shards, dtype=jnp.int32) // groups
    selector = (owners[:, None] == jnp.arange(KVH, dtype=jnp.int32)[None, :]).astype(jnp.bfloat16)
    placed = jnp.einsum(
        "tnc,nh->thc",
        piece.reshape(count, shards, pair_width),
        selector,
        preferred_element_type=jnp.float32,
    )
    grads_all = placed.reshape(count, kv_width).astype(jnp.bfloat16)
    fisher = seq_fisher(inputs, grads_all, owner, starts, lengths.shape[1])
    weighted = fisher * task_weights[0].astype(jnp.float32)
    weighted_sum, fisher_sum = (
        lax.psum(weighted.astype(jnp.bfloat16), "task").astype(jnp.float32),
        lax.psum(fisher.astype(jnp.bfloat16), "task").astype(jnp.float32),
    )
    merged = (weighted_sum / (fisher_sum + EPS)).astype(jnp.bfloat16)
    return (fisher[None], merged)


def solution(mesh):
    in_specs = (
        P("task", None, "col"),
        P("task", None, "col"),
        P("task", "col", None),
        P("task", None, "col"),
        P("task", None),
        P("task", "col", None),
    )
    out_specs = (P("task", "col", None), P("col", None))
    return jax.shard_map(body, mesh=mesh, in_specs=in_specs, out_specs=out_specs, check_vma=False)
```

profile of v0, /device:TPU:0, one launch (start us, length us, event | category | flops | bytes accessed | tf_op | source)
XLA Modules:
  0.0 478.3 jit_solution(18037446713357013395)
XLA Ops:
  7.2 2.2 copy.13
  9.4 7.3 %all-to-all-start = ((bf16[128,8,256]{0,2,1:T(8,128)(2,1)}), bf16[128,8,256]{0,2,1:T(8,128)(2,1)S(1)}, u32[]{:S(2)}, u32[]{:S(2)}) async-start(bf16[128,8,256]{0,2,1:T(8,128)(2,1)} %bitcast.6), calls=%async_computation | async-start | bytes 1048576 | tf_op jit(solution)/shard_map/all_to_all | solution.py:67
  17.6 13.5 %all-to-all-done = bf16[128,8,256]{0,2,1:T(8,128)(2,1)S(1)} async-done(((bf16[128,8,256]{0,2,1:T(8,128)(2,1)}), bf16[128,8,256]{0,2,1:T(8,128)(2,1)S(1)}, u32[]{:S(2)}, u32[]{:S(2)}) %all-to-all-start) | async-done | bytes 524320 | tf_op jit(solution)/shard_map/all_to_all | solution.py:67
  31.4 3.6 fusion.104
  34.9 2.7 fusion.98
  37.6 2.6 fusion.92
  40.3 2.8 fusion.86
  43.8 2.7 fusion.74
  47.2 2.7 fusion.101
  49.9 2.7 fusion.95
  52.5 2.6 fusion.89
  55.2 2.7 fusion.107
  59.2 3.0 exponential_reduce_fusion
  64.5 15.9 %multiply_reduce_fusion = (f32[1024]{0:T(1024)S(1)}, f32[1024]{0:T(1024)S(1)}, f32[1024]{0:T(1024)S(1)}, f32[1024]{0:T(1024)S(1)}, f32[1024]{0:T(1024)S(1)}, /*i...) fusion(f32[1024]{0:T(1024)S(1)} %log.71, f32[1024]{0:T(1024)S(1)} %get-tuple-element.74, ...), kind=kOutput, calls=%fused_computation.13 | convolution fusion | flops 305127424 | bytes 42524672 | tf_op jit(solution)/shard_map/dot_general | solution.py:30
  80.3 1.7 exponential_reduce_fusion.2
  82.1 2.2 fusion.31
  85.6 8.4 %exponential_reduce_fusion.1 = (f32[1024]{0:T(1024)S(1)}, f32[1024]{0:T(1024)S(1)}, f32[1024]{0:T(1024)S(1)}, f32[1024]{0:T(1024)S(1)}, f32[1024]{0:T(1024)S(1)}, /*index=5*/f32[1024,1024]{0,1:T(8,128)}) fusion(f32[1024,1024]{0,1:T(8,128)S(1)} %copy-done.4, f32[1024]{0:T(1024)S(1)} %get-tuple-element.71, s32[1024]{0:T(1024)S(1)} %convert_reduce_fusion, ...), kind=kOutput, calls=%fused_computation.20 | convolution fusion | flops 295693312 | bytes 25743360 | tf_op jit(solution)/shard_map/dot_general | solution.py:30
  94.0 2.1 fusion.37
  96.1 4.2 fusion.40
  100.3 3.9 fusion.43
  104.2 4.1 fusion.28
  108.3 15.3 %multiply_reduce_fusion.1 = (f32[1024]{0:T(1024)S(1)}, f32[1024]{0:T(1024)S(1)}, f32[1024]{0:T(1024)S(1)}, f32[1024]{0:T(1024)S(1)}, f32[1024]{0:T(1024)S(1)}, /*index=5*/f32[1024,1024]{0,1:T(8,128)}) fusion(f32[1024]{0:T(1024)S(1)} %log.70, f32[1024]{0:T(1024)S(1)} %get-tuple-element.71, f32[1024,1024]{0,1:T(8,128)} %fusion.74, ...), kind=kOutput, calls=%fused_computation.18 | convolution fusion | flops 305130496 | bytes 38338560 | tf_op jit(solution)/shard_map/dot_general | solution.py:30
  123.6 2.1 fusion.34
  125.7 4.9 %multiply_reduce_fusion.3 = (f32[1024]{0:T(1024)S(1)}, f32[1024,1024]{0,1:T(8,128)}) fusion(f32[1024]{0:T(1024)S(1)} %log.68, f32[1024]{0:T(1024)S(1)} %get-tuple-element.69, f32[1024,1024]{0,1:T(8,128)S(1)} %copy-done.3, s32[1024]{0:T(1024)S(1)} %convert_reduce_fusion, bf16[1024,256]{1,0:T(8,128)(2,1)S(1)} %bitcast.48, bf16[1024,1024]{1,0:T(8,128)(2,1)} %bitcast.78), kind=kOutput, calls=%fused_computation.28 | convolution fusion | flops 278920192 | bytes 8933376 | tf_op jit(solution)/shard_map/dot_general | solution.py:30
  130.7 1.5 fusion.56
  132.8 1.3 copy-done.14
  134.1 1.5 fusion.53
  137.6 1.5 fusion.54
  141.0 1.5 fusion.55
  143.2 1.3 copy-done.23
  144.5 1.5 fusion.49
  146.7 1.5 fusion.51
  148.9 1.3 copy-done.25
  150.2 1.5 fusion.50
  152.4 1.7 fusion.52
  154.1 1.6 fusion.63
  155.9 71.9 %all-gather.2.cloned.1.call-done = bf16[1024,2048]{0,1:T(8,128)(2,1)} async-done(((bf16[1024,256]{0,1:T(8,128)(2,1)}), bf16[1024,2048]{0,1:T(8,128)(2,1)}) %all-gather.2.cloned.1.call-update) | async-done | bytes 4194320 | tf_op jit(solution)/shard_map/all_gather | solution.py:83
  227.8 6.9 %copy.15 = bf16[1024,8,256]{2,1,0:T(8,128)(2,1)} copy(bf16[1024,8,256]{0,2,1:T(8,128)(2,1)} %bitcast.51) | data formatting | bytes 8388608 | tf_op jit(solution)/shard_map/reshape | solution.py:89
  234.7 3.4 convolution_convert_fusion
  238.1 3.5 copy.16
  241.6 57.4 %while.11 = (s32[]{:T(128)}, f32[1024,2048]{1,0:T(8,128)}, s32[4]{0:T(128)S(1)}, s32[4]{0:T(128)S(1)}, bf16[1024,1024]{1,0:T(8,128)(2,1)S(1)}, /*index=5*/s32[10...) while((s32[]{:T(128)}, f32[1024,2048]{1,0:T(8,128)}, ...), condition=%wide.region_27.28_spmd.clone, body=%wide.region_26.27_spmd.clone.sunk | while | flops 2154824192 | bytes 19927264 | solution.py:54
  246.2 7.9 %select_add_fusion.2 = f32[1024,2048]{1,0:T(8,128)} fusion(f32[1024,2048]{1,0:T(8,128)} %get-tuple-element.166, pred[]{:T(512)S(6)} %compare.5, bf16[1024,2048]{1,0:T(8,128)(2,1)} %get-tuple-element.183, s32[]{:T(128)} %bitcast.30, pred[512]{0:T(512)(128)(4,1)S(1)} %dynamic-slice_compare_fusion.2, bf16[1024,1024]{1,0:T(8,128)(2,1)S(1)} %get-tuple-element.181), kind=kOutput, calls=%fused_computation.clone.1 | convolution fusion | flops 2154823680 | bytes 19924480 | tf_op jit(solution)/shard_map/while/body/eval_jaxpr/dot_general | solution.py:50
  258.8 10.3 %select_add_fusion.2 = f32[1024,2048]{1,0:T(8,128)} fusion(f32[1024,2048]{1,0:T(8,128)} %get-tuple-element.166, pred[]{:T(512)S(6)} %compare.5, bf16[1024,2048]{1,0:T(8,128)(2,1)} %get-tuple-element.183, s32[]{:T(128)} %bitcast.30, pred[512]{0:T(512)(128)(4,1)S(1)} %dynamic-slice_compare_fusion.2, bf16[1024,1024]{1,0:T(8,128)(2,1)S(1)} %get-tuple-element.181), kind=kOutput, calls=%fused_computation.clone.1 | convolution fusion | flops 2154823680 | bytes 19924480 | tf_op jit(solution)/shard_map/while/body/eval_jaxpr/dot_general | solution.py:50
  273.8 10.3 %select_add_fusion.2 = f32[1024,2048]{1,0:T(8,128)} fusion(f32[1024,2048]{1,0:T(8,128)} %get-tuple-element.166, pred[]{:T(512)S(6)} %compare.5, bf16[1024,2048]{1,0:T(8,128)(2,1)} %get-tuple-element.183, s32[]{:T(128)} %bitcast.30, pred[512]{0:T(512)(128)(4,1)S(1)} %dynamic-slice_compare_fusion.2, bf16[1024,1024]{1,0:T(8,128)(2,1)S(1)} %get-tuple-element.181), kind=kOutput, calls=%fused_computation.clone.1 | convolution fusion | flops 2154823680 | bytes 19924480 | tf_op jit(solution)/shard_map/while/body/eval_jaxpr/dot_general | solution.py:50
  288.7 10.3 %select_add_fusion.2 = f32[1024,2048]{1,0:T(8,128)} fusion(f32[1024,2048]{1,0:T(8,128)} %get-tuple-element.166, pred[]{:T(512)S(6)} %compare.5, bf16[1024,2048]{1,0:T(8,128)(2,1)} %get-tuple-element.183, s32[]{:T(128)} %bitcast.30, pred[512]{0:T(512)(128)(4,1)S(1)} %dynamic-slice_compare_fusion.2, bf16[1024,1024]{1,0:T(8,128)(2,1)S(1)} %get-tuple-element.181), kind=kOutput, calls=%fused_computation.clone.1 | convolution fusion | flops 2154823680 | bytes 19924480 | tf_op jit(solution)/shard_map/while/body/eval_jaxpr/dot_general | solution.py:50
  299.0 12.8 %fusion.7 = (bf16[1024,2048]{1,0:T(8,128)(2,1)}, bf16[1024,2048]{1,0:T(8,128)(2,1)}) fusion(f32[1024,2048]{1,0:T(8,128)} %get-tuple-element.39, bf16[1,1024,2048]{2,1,0:T(8,128)(2,1)} %param.13), kind=kLoop, calls=%fused_computation.10 | loop fusion | flops 8388608 | bytes 20971520 | tf_op jit(solution)/shard_map/convert_element_type | solution.py:97
  311.8 151.6 %all-reduce.3.cloned.1.call-done = (bf16[1024,2048]{1,0:T(8,128)(2,1)}, bf16[1024,2048]{1,0:T(8,128)(2,1)}) async-done(((bf16[1024,2048]{1,0:T(8,128)(2,1)}, bf16[1024,2048]{1,0:T(8,128)(2,1)}), (bf16[1024,2048]{1,0:T(8,128)(2,1)}, bf16[1024,2048]{1,0:T(8,128)(2,1)})) %all-reduce.3.cloned.1.call-update) | async-done | bytes 8388624 | tf_op jit(solution)/shard_map/psum | solution.py:98
  463.4 7.9 %divide_convert_fusion = bf16[1024,2048]{1,0:T(8,128)(2,1)} fusion(bf16[1024,2048]{1,0:T(8,128)(2,1)} %get-tuple-element.100, bf16[1024,2048]{1,0:T(8,128)(2,1)} %get-tuple-element.101), kind=kLoop, calls=%fused_computation.11 | loop fusion | flops 10485760 | bytes 12582912 | tf_op jit(solution)/shard_map/convert_element_type | solution.py:100
  (84 shorter events, 22.9 us)
Async XLA Ops:
  7.2 27.8 %copy-start.16 = (bf16[1,1024,1024]{2,1,0:T(8,128)(2,1)S(1)}, bf16[1,1024,1024]{2,1,0:T(8,128)(2,1)}, u32[]{:S(2)}) copy-start(bf16[1,1024,1024]{2,1,0:T(8,128)(2,1)} %param.9) | copy-start | bytes 6291460
  9.4 21.8 %all-to-all-start = ((bf16[128,8,256]{0,2,1:T(8,128)(2,1)}), bf16[128,8,256]{0,2,1:T(8,128)(2,1)S(1)}, u32[]{:S(2)}, u32[]{:S(2)}) async-start(bf16[128,8,256]{0,2,1:T(8,128)(2,1)} %bitcast.6), calls=%async_computation | async-start | bytes 1048576 | tf_op jit(solution)/shard_map/all_to_all | solution.py:67
  16.6 211.2 %all-gather.2.cloned.1.call-start = ((), (), s32[]{:S(2)}) async-start(), calls=%async_computation.1 | async-start | bytes 4718592 | tf_op jit(solution)/shard_map/all_gather | solution.py:83
  43.8 3.4 copy-start.17
  59.2 4.1 copy-start.1
  80.3 4.0 copy-start.9
  82.0 2.4 copy-start.4
  82.0 3.6 copy-start.6
  85.6 8.4 %copy-start.12 = (f32[1024,1024]{0,1:T(8,128)S(1)}, f32[1024,1024]{0,1:T(8,128)}, u32[]{:S(2)}) copy-start(f32[1024,1024]{0,1:T(8,128)} %fusion.92) | copy-start | bytes 12582916
  104.2 4.1 copy-start.3
  125.7 4.9 %copy-start.15 = (f32[1024,1024]{0,1:T(8,128)S(1)}, f32[1024,1024]{0,1:T(8,128)}, u32[]{:S(2)}) copy-start(f32[1024,1024]{0,1:T(8,128)} %fusion.107) | copy-start | bytes 12582916
  130.6 2.2 copy-start.13
  130.7 3.5 copy-start.14
  134.1 2.2 copy-start.10
  134.1 3.5 copy-start.11
  137.6 2.2 copy-start.7
  137.6 3.5 copy-start.8
  141.0 2.2 copy-start.2
  141.0 3.5 copy-start.23
  144.5 2.2 copy-start.24
  146.7 2.2 copy-start.5
  146.7 3.5 copy-start.25
  150.2 2.2 copy-start.22
  152.4 1.7 copy-start.18
  152.4 1.7 copy-start.19
  152.4 1.7 copy-start.20
  154.1 1.7 copy-start.21
  155.8 307.6 %all-reduce.3.cloned.1.call-start = ((), (), s32[]{:S(2)}) async-start(), calls=%async_computation.2 | async-start | bytes 16777216 | tf_op jit(solution)/shard_map/psum | solution.py:98
  238.1 3.5 copy-start
Sparse Core Ops, SparseCore 0:
  155.9 71.8 all-gather.1
  312.0 151.3 all-reduce.2
where the time goes:
time: 486 us; the launch traced here: 478 us
  waiting for transfers between devices  237 us (49%)
  matrix products  148 us (30%)
  other arithmetic  31 us (6%)
  local copies, waits for them, and re-layouts  30.2 us (6%)
  between operations  14.6 us (3%)
  loops' own time  10.6 us (2%)
  starting transfers between devices  7.36 us (2%)
    psum x1, waiting for transfers between devices, body(): lax.psum(fisher.astype(jnp.bfloat16), 'task').astype(jnp.float32)  152 us
    all_gather x1, waiting for transfers between devices, body(): piece = lax.all_gather(partial_value, 'col', axis=1, tiled=True)  71.9 us
    dot_general x8, matrix products, head_grads(): jnp.dot(head_cotangent, head_values.T, preferred_element_type=jnp.float32)  55.1 us
    dot_general x4, matrix products, one_seq(): gradient = jnp.dot(rows_in.T, rows_grad, preferred_element_type=jnp.float32)  38.8 us
    dot_general x8, matrix products, head_grads(): jnp.dot(chances.astype(jnp.bfloat16).T, head_cotangent, preferred_element...  20.8 us
    unnamed x54, local copies, waits for them, and re-layouts  18.1 us
    dot_general x8, matrix products, head_grads(): jnp.dot(head_query, head_keys.T, preferred_element_type=jnp.float32)  17.1 us
    all_to_all x1, waiting for transfers between devices, body(): lax.all_to_all(copies, 'col', split_axis=1, concat_axis=0, tiled=True)  13.5 us
  transfers between devices with their start and end apart: 3, of which 3 were waited for; matrix products, arithmetic and copies ran while one was open for 0% of the time, Pallas kernels for 0%

commit v1 on v0

--- a/solution.py
+++ b/solution.py
@@ -95,7 +95,7 @@
     weighted = fisher * task_weights[0].astype(jnp.float32)
     weighted_sum, fisher_sum = (
         lax.psum(weighted.astype(jnp.bfloat16), "task").astype(jnp.float32),
-        lax.psum(fisher.astype(jnp.bfloat16), "task").astype(jnp.float32),
+        jnp.sum(lax.all_gather(fisher.astype(jnp.bfloat16), "task"), axis=0).astype(jnp.float32),
     )
     merged = (weighted_sum / (fisher_sum + EPS)).astype(jnp.bfloat16)
     return (fisher[None], merged)

time: 486 us -> 527 us (1.084)
  waiting for transfers between devices: 237 us -> 266 us
  other arithmetic: 31 us -> 43.8 us
    all_gather x0 -> x1, waiting for transfers between devices: none -> 104 us  [body(): lax.all_gather(fisher.astype(jnp.bfloat16), 'task')]
    psum x1, waiting for transfers between devices: 152 us -> 75.7 us  [body(): lax.psum(weighted.astype(jnp.bfloat16), 'task').astype(jnp.float32)]
    reduce_sum x0 -> x1, other arithmetic: none -> 12.8 us  [body(): jnp.sum(lax.all_gather(fisher.astype(jnp.bfloat16), 'task'), axis=0)]
  transfers between devices with their start and end apart: 3 -> 4, of which waited for: 3 -> 4; matrix products, arithmetic and copies ran while one was open for 0% -> 3% of each run, Pallas kernels for 0% -> 0%
where the time goes in v1:
time: 527 us; the launch traced here: 520 us
  waiting for transfers between devices  266 us (50%)
  matrix products  148 us (28%)
  other arithmetic  43.8 us (8%)
  local copies, waits for them, and re-layouts  30.2 us (6%)
  between operations  14.3 us (3%)
  loops' own time  10.6 us (2%)
  starting transfers between devices  7.4 us (1%)
    all_gather x1, waiting for transfers between devices, body(): lax.all_gather(fisher.astype(jnp.bfloat16), 'task')  104 us
    psum x1, waiting for transfers between devices, body(): lax.psum(weighted.astype(jnp.bfloat16), 'task').astype(jnp.float32)  75.7 us
    all_gather x1, waiting for transfers between devices, body(): piece = lax.all_gather(partial_value, 'col', axis=1, tiled=True)  71.9 us
    dot_general x8, matrix products, head_grads(): jnp.dot(head_cotangent, head_values.T, preferred_element_type=jnp.float32)  55.1 us
    dot_general x4, matrix products, one_seq(): gradient = jnp.dot(rows_in.T, rows_grad, preferred_element_type=jnp.float32)  38.8 us
    dot_general x8, matrix products, head_grads(): jnp.dot(chances.astype(jnp.bfloat16).T, head_cotangent, preferred_element...  20.8 us
    unnamed x54, local copies, waits for them, and re-layouts  18.1 us
    dot_general x8, matrix products, head_grads(): jnp.dot(head_query, head_keys.T, preferred_element_type=jnp.float32)  17.1 us
  transfers between devices with their start and end apart: 4, of which 4 were waited for; matrix products, arithmetic and copies ran while one was open for 3% of the time, Pallas kernels for 0%

profile of v1, /device:TPU:0, one launch (start us, length us, event | category | flops | bytes accessed | tf_op | source)
XLA Modules:
  0.0 519.6 jit_solution(5383115996678895686)
XLA Ops:
  7.2 2.2 copy.13
  9.4 7.3 %all-to-all-start = ((bf16[128,8,256]{0,2,1:T(8,128)(2,1)}), bf16[128,8,256]{0,2,1:T(8,128)(2,1)S(1)}, u32[]{:S(2)}, u32[]{:S(2)}) async-start(bf16[128,8,256]{0,2,1:T(8,128)(2,1)} %bitcast.6), calls=%async_computation | async-start | bytes 1048576 | tf_op jit(solution)/shard_map/all_to_all | solution.py:67
  17.6 13.5 %all-to-all-done = bf16[128,8,256]{0,2,1:T(8,128)(2,1)S(1)} async-done(((bf16[128,8,256]{0,2,1:T(8,128)(2,1)}), bf16[128,8,256]{0,2,1:T(8,128)(2,1)S(1)}, u32[]{:S(2)}, u32[]{:S(2)}) %all-to-all-start) | async-done | bytes 524320 | tf_op jit(solution)/shard_map/all_to_all | solution.py:67
  31.4 3.6 fusion.104
  34.9 2.7 fusion.98
  37.6 2.6 fusion.92
  40.3 2.8 fusion.86
  43.8 2.7 fusion.74
  47.2 2.7 fusion.101
  49.9 2.7 fusion.95
  52.5 2.6 fusion.89
  55.2 2.7 fusion.107
  59.2 3.0 exponential_reduce_fusion
  64.5 15.9 %multiply_reduce_fusion = (f32[1024]{0:T(1024)S(1)}, f32[1024]{0:T(1024)S(1)}, f32[1024]{0:T(1024)S(1)}, f32[1024]{0:T(1024)S(1)}, f32[1024]{0:T(1024)S(1)}, /*i...) fusion(f32[1024]{0:T(1024)S(1)} %log.71, f32[1024]{0:T(1024)S(1)} %get-tuple-element.74, ...), kind=kOutput, calls=%fused_computation.13 | convolution fusion | flops 305127424 | bytes 42524672 | tf_op jit(solution)/shard_map/dot_general | solution.py:30
  80.3 1.7 exponential_reduce_fusion.2
  82.1 2.2 fusion.31
  85.6 8.4 %exponential_reduce_fusion.1 = (f32[1024]{0:T(1024)S(1)}, f32[1024]{0:T(1024)S(1)}, f32[1024]{0:T(1024)S(1)}, f32[1024]{0:T(1024)S(1)}, f32[1024]{0:T(1024)S(1)}, /*index=5*/f32[1024,1024]{0,1:T(8,128)}) fusion(f32[1024,1024]{0,1:T(8,128)S(1)} %copy-done.4, f32[1024]{0:T(1024)S(1)} %get-tuple-element.71, s32[1024]{0:T(1024)S(1)} %convert_reduce_fusion, ...), kind=kOutput, calls=%fused_computation.20 | convolution fusion | flops 295693312 | bytes 25743360 | tf_op jit(solution)/shard_map/dot_general | solution.py:30
  94.0 2.1 fusion.37
  96.1 4.2 fusion.40
  100.3 3.9 fusion.43
  104.2 4.1 fusion.28
  108.3 15.3 %multiply_reduce_fusion.1 = (f32[1024]{0:T(1024)S(1)}, f32[1024]{0:T(1024)S(1)}, f32[1024]{0:T(1024)S(1)}, f32[1024]{0:T(1024)S(1)}, f32[1024]{0:T(1024)S(1)}, /*index=5*/f32[1024,1024]{0,1:T(8,128)}) fusion(f32[1024]{0:T(1024)S(1)} %log.70, f32[1024]{0:T(1024)S(1)} %get-tuple-element.71, f32[1024,1024]{0,1:T(8,128)} %fusion.74, ...), kind=kOutput, calls=%fused_computation.18 | convolution fusion | flops 305130496 | bytes 38338560 | tf_op jit(solution)/shard_map/dot_general | solution.py:30
  123.6 2.1 fusion.34
  125.7 4.9 multiply_reduce_fusion.3
  130.7 1.5 fusion.56
  132.8 1.3 copy-done.14
  134.1 1.5 fusion.53
  137.6 1.5 fusion.54
  141.0 1.5 fusion.55
  144.5 1.5 fusion.49
  146.7 1.5 fusion.51
  150.2 1.5 fusion.50
  152.4 1.7 fusion.52
  154.1 1.6 fusion.63
  155.9 71.9 %all-gather.4.cloned.1.call-done = bf16[1024,2048]{0,1:T(8,128)(2,1)} async-done(((bf16[1024,256]{0,1:T(8,128)(2,1)}), bf16[1024,2048]{0,1:T(8,128)(2,1)}) %all-gather.4.cloned.1.call-update) | async-done | bytes 4194320 | tf_op jit(solution)/shard_map/all_gather | solution.py:83
  227.8 6.9 %copy.15 = bf16[1024,8,256]{2,1,0:T(8,128)(2,1)} copy(bf16[1024,8,256]{0,2,1:T(8,128)(2,1)} %bitcast.53) | data formatting | bytes 8388608 | tf_op jit(solution)/shard_map/reshape | solution.py:89
  234.7 3.4 convolution_convert_fusion
  238.1 3.5 copy.16
  241.6 57.4 %while.11 = (s32[]{:T(128)}, f32[1024,2048]{1,0:T(8,128)}, s32[4]{0:T(128)S(1)}, s32[4]{0:T(128)S(1)}, bf16[1024,1024]{1,0:T(8,128)(2,1)S(1)}, /*index=5*/s32[10...) while((s32[]{:T(128)}, f32[1024,2048]{1,0:T(8,128)}, ...), condition=%wide.region_27.28_spmd.clone, body=%wide.region_26.27_spmd.clone.sunk | while | flops 2154824192 | bytes 19927264 | solution.py:54
  246.2 7.9 %select_add_fusion.2 = f32[1024,2048]{1,0:T(8,128)} fusion(f32[1024,2048]{1,0:T(8,128)} %get-tuple-element.164, pred[]{:T(512)S(6)} %compare.5, bf16[1024,2048]{1,0:T(8,128)(2,1)} %get-tuple-element.181, s32[]{:T(128)} %bitcast.31, pred[512]{0:T(512)(128)(4,1)S(1)} %dynamic-slice_compare_fusion.2, bf16[1024,1024]{1,0:T(8,128)(2,1)S(1)} %get-tuple-element.179), kind=kOutput, calls=%fused_computation.clone.1 | convolution fusion | flops 2154823680 | bytes 19924480 | tf_op jit(solution)/shard_map/while/body/eval_jaxpr/dot_general | solution.py:50
  258.8 10.3 %select_add_fusion.2 = f32[1024,2048]{1,0:T(8,128)} fusion(f32[1024,2048]{1,0:T(8,128)} %get-tuple-element.164, pred[]{:T(512)S(6)} %compare.5, bf16[1024,2048]{1,0:T(8,128)(2,1)} %get-tuple-element.181, s32[]{:T(128)} %bitcast.31, pred[512]{0:T(512)(128)(4,1)S(1)} %dynamic-slice_compare_fusion.2, bf16[1024,1024]{1,0:T(8,128)(2,1)S(1)} %get-tuple-element.179), kind=kOutput, calls=%fused_computation.clone.1 | convolution fusion | flops 2154823680 | bytes 19924480 | tf_op jit(solution)/shard_map/while/body/eval_jaxpr/dot_general | solution.py:50
  273.8 10.3 %select_add_fusion.2 = f32[1024,2048]{1,0:T(8,128)} fusion(f32[1024,2048]{1,0:T(8,128)} %get-tuple-element.164, pred[]{:T(512)S(6)} %compare.5, bf16[1024,2048]{1,0:T(8,128)(2,1)} %get-tuple-element.181, s32[]{:T(128)} %bitcast.31, pred[512]{0:T(512)(128)(4,1)S(1)} %dynamic-slice_compare_fusion.2, bf16[1024,1024]{1,0:T(8,128)(2,1)S(1)} %get-tuple-element.179), kind=kOutput, calls=%fused_computation.clone.1 | convolution fusion | flops 2154823680 | bytes 19924480 | tf_op jit(solution)/shard_map/while/body/eval_jaxpr/dot_general | solution.py:50
  288.7 10.3 %select_add_fusion.2 = f32[1024,2048]{1,0:T(8,128)} fusion(f32[1024,2048]{1,0:T(8,128)} %get-tuple-element.164, pred[]{:T(512)S(6)} %compare.5, bf16[1024,2048]{1,0:T(8,128)(2,1)} %get-tuple-element.181, s32[]{:T(128)} %bitcast.31, pred[512]{0:T(512)(128)(4,1)S(1)} %dynamic-slice_compare_fusion.2, bf16[1024,1024]{1,0:T(8,128)(2,1)S(1)} %get-tuple-element.179), kind=kOutput, calls=%fused_computation.clone.1 | convolution fusion | flops 2154823680 | bytes 19924480 | tf_op jit(solution)/shard_map/while/body/eval_jaxpr/dot_general | solution.py:50
  299.0 12.8 %fusion.7 = (bf16[1024,2048]{1,0:T(8,128)(2,1)}, bf16[1024,2048]{1,0:T(8,128)(2,1)}) fusion(f32[1024,2048]{1,0:T(8,128)} %get-tuple-element.39, bf16[1,1024,2048]{2,1,0:T(8,128)(2,1)} %param.13), kind=kLoop, calls=%fused_computation.10 | loop fusion | flops 8388608 | bytes 20971520 | tf_op jit(solution)/shard_map/convert_element_type | solution.py:97
  312.6 103.8 %all-gather.6.cloned.1.call-done = bf16[4096,2048]{1,0:T(8,128)(2,1)} async-done(((bf16[1024,2048]{1,0:T(8,128)(2,1)}), bf16[4096,2048]{1,0:T(8,128)(2,1)}) %all-gather.6.cloned.1.call-update) | async-done | bytes 16777232 | tf_op jit(solution)/shard_map/all_gather | solution.py:98
  416.4 12.8 %reduce_sum.182 = bf16[1024,2048]{1,0:T(8,128)(2,1)} reduce(bf16[4,1024,2048]{2,1,0:T(8,128)(2,1)} %bitcast.50, bf16[]{:T(256)} %constant.46.clone.1), dimensions={0}, to_apply=%region_29.30 | reduce | flops 6291456 | bytes 20971522 | tf_op jit(solution)/shard_map/reduce_sum | solution.py:98
  429.2 75.7 %all-reduce.2.cloned.1.call-done = bf16[1024,2048]{1,0:T(8,128)(2,1)} async-done(((bf16[1024,2048]{1,0:T(8,128)(2,1)}), bf16[1024,2048]{1,0:T(8,128)(2,1)}) %all-reduce.2.cloned.1.call-update) | async-done | bytes 4194320 | tf_op jit(solution)/shard_map/psum | solution.py:97
  504.9 7.9 %divide_convert_fusion = bf16[1024,2048]{1,0:T(8,128)(2,1)} fusion(bf16[1024,2048]{1,0:T(8,128)(2,1)} %reduce_sum.182, bf16[1024,2048]{1,0:T(8,128)(2,1)} %all-reduce.2.cloned.1.call-done), kind=kLoop, calls=%fused_computation.11 | loop fusion | flops 10485760 | bytes 12582912 | tf_op jit(solution)/shard_map/convert_element_type | solution.py:100
  (88 shorter events, 26.1 us)
Async XLA Ops:
  7.2 27.8 %copy-start.16 = (bf16[1,1024,1024]{2,1,0:T(8,128)(2,1)S(1)}, bf16[1,1024,1024]{2,1,0:T(8,128)(2,1)}, u32[]{:S(2)}) copy-start(bf16[1,1024,1024]{2,1,0:T(8,128)(2,1)} %param.9) | copy-start | bytes 6291460
  9.4 21.8 %all-to-all-start = ((bf16[128,8,256]{0,2,1:T(8,128)(2,1)}), bf16[128,8,256]{0,2,1:T(8,128)(2,1)S(1)}, u32[]{:S(2)}, u32[]{:S(2)}) async-start(bf16[128,8,256]{0,2,1:T(8,128)(2,1)} %bitcast.6), calls=%async_computation | async-start | bytes 1048576 | tf_op jit(solution)/shard_map/all_to_all | solution.py:67
  16.6 211.2 %all-gather.4.cloned.1.call-start = ((), (), s32[]{:S(2)}) async-start(), calls=%async_computation.1 | async-start | bytes 4718592 | tf_op jit(solution)/shard_map/all_gather | solution.py:83
  43.7 3.4 copy-start.17
  59.2 4.1 copy-start.1
  80.3 4.0 copy-start.9
  82.0 2.4 copy-start.4
  82.0 3.6 copy-start.6
  85.6 8.4 %copy-start.12 = (f32[1024,1024]{0,1:T(8,128)S(1)}, f32[1024,1024]{0,1:T(8,128)}, u32[]{:S(2)}) copy-start(f32[1024,1024]{0,1:T(8,128)} %fusion.92) | copy-start | bytes 12582916
  104.2 4.1 copy-start.3
  125.7 4.9 copy-start.15
  130.6 2.2 copy-start.13
  130.7 3.5 copy-start.14
  134.1 2.2 copy-start.10
  134.1 3.5 copy-start.11
  137.6 2.2 copy-start.7
  137.6 3.5 copy-start.8
  141.0 2.2 copy-start.2
  141.0 3.5 copy-start.23
  144.5 2.2 copy-start.24
  146.7 2.2 copy-start.5
  146.7 3.5 copy-start.25
  150.2 2.2 copy-start.22
  152.4 1.7 copy-start.18
  152.4 1.7 copy-start.19
  152.4 1.7 copy-start.20
  154.1 1.7 copy-start.21
  155.8 260.6 %all-gather.6.cloned.1.call-start = ((), (), s32[]{:S(2)}) async-start(), calls=%async_computation.3 | async-start | bytes 20971520 | tf_op jit(solution)/shard_map/all_gather | solution.py:98
  238.1 3.5 copy-start
  311.8 193.1 %all-reduce.2.cloned.1.call-start = ((), (), s32[]{:S(2)}) async-start(), calls=%async_computation.2 | async-start | bytes 8388608 | tf_op jit(solution)/shard_map/psum | solution.py:97
Sparse Core Ops, SparseCore 0:
  155.9 71.8 all-gather.3
  311.9 104.4 all-gather.5
  419.4 85.4 all-reduce.1
